TPU v7x, 512 devices: a 4x2x32 block of a 4x8x32 slice. The times are simulated.
512 devices in a mesh: group: 2 (over y), expert: 64 (over z, core), tensor: 4 (over x).
Axes of the slice: x: 4, y: 2, z: 32, core: 2. Of those that a mesh axis runs over, the one named last changes fastest.
The devices are a block of a 4x8x32 slice.
Arguments:
- tokens: bfloat16 [4096, 4096], P(('group', 'expert'), 'tensor'), parts along dimension 0, may hold values from -6 to 6
- expert_ids: int32 [4096, 8], P(('group', 'expert')), parts along dimension 0, may hold values from 0 to 63, all different within a row; in each aligned block of 32 rows (0 to 31, 32 to 63, ...) at most 6 rows name the same one
- router_logits: float32 [4096, 8], P(('group', 'expert')), parts along dimension 0, may hold values from -6 to 6
- up_weight: bfloat16 [64, 4096, 1024], P('expert', None, 'tensor'), may hold values from -0.09375 to 0.09375
- down_weight: bfloat16 [64, 1024, 4096], P('expert', 'tensor'), may hold values from -0.1875 to 0.1875
Outputs:
- moe_out: bfloat16 [4096, 4096], P(('group', 'expert'), 'tensor'), parts along dimension 0
There are 2 independent parts, one for each index of `group`. A program takes and returns all parts, laid end to end along the dimension named above; an argument that names none is the same for every part. Nothing has to cross between parts.
Inputs may be any that keep to these rules, and one draw needn't show every extreme that they name: `expert_ids`: each row names 8 different experts. In each aligned block of 32 rows (the rows of one index of the expert axis) no expert is named by more than 6 rows, a bound that some block reaches.
All inputs are finite; a program needn't handle non-finite values.
Results may differ from a plain program's by a relative error of at most 0.014.
Values may be sent and summed in bfloat16 or wider, within the bound.
No kernel may reach another device: no remote copies, remote signals or barrier semaphores. Data moves between devices by JAX's collectives and lax.ppermute only.
A program may use at most 64 MiB of HBM per device.

v0:
```python
import jax
import jax.numpy as jnp
from jax import lax
from jax.sharding import Mesh
from jax.sharding import PartitionSpec as P

EXPERT = ("expert_0", "expert_1")
GROUP_EXPERT = ("group", "expert_0", "expert_1")


def in_blocks(shard, dim, count):
    shape = shard.shape
    pieces = shard.reshape(*shape[:dim], count, shape[dim] // count, *shape[dim + 1 :])
    return jnp.moveaxis(pieces, dim, 0)


def joined_along(pieces, dim):
    shape = list(pieces.shape[1:])
    shape[dim] *= pieces.shape[0]
    return jnp.moveaxis(pieces, 0, dim).reshape(shape)


def exchange_in_order(pieces, axes, order):
    shape = [lax.axis_size(a) for a in axes]
    pieces = pieces.reshape(*shape, *pieces.shape[1:])
    for k in order:
        pieces = lax.all_to_all(pieces, axes[k], split_axis=k, concat_axis=k, tiled=True)
    return pieces.reshape(-1, *pieces.shape[len(axes) :])


def core_and_chips(shard, groups, order, split_dim, concat_dim):
    count = lax.axis_size(groups[0]) * lax.axis_size(groups[1])
    pieces = in_blocks(shard, split_dim, count)
    return joined_along(exchange_in_order(pieces, groups, order), concat_dim)


def summed_on_arrival(shard, axis, dim):
    count = lax.axis_size(axis)
    pieces = lax.all_to_all(in_blocks(shard, dim, count), axis, 0, 0, tiled=True)
    return jnp.sum(pieces.astype(jnp.float32), axis=0)


def on_device(tokens, expert_ids, router_logits, up_weight, down_weight):
    tok_rows = tokens.shape[0]
    quarter_width = tokens.shape[1]
    top_count = expert_ids.shape[1]
    experts = lax.axis_size(EXPERT)
    capacity = max(2, 3 * tok_rows * top_count // (2 * experts))
    hits = (expert_ids[:, :, None] == jnp.arange(experts, dtype=jnp.int32)[None, None, :]).astype(
        jnp.int32
    )
    per_token = jnp.sum(hits, axis=1)
    rank = jnp.cumsum(per_token, axis=0) - per_token
    slot = jnp.sum(hits * rank[:, None, :], axis=2)
    position = expert_ids * capacity + slot
    placing = position[:, :, None] == jnp.arange(experts * capacity, dtype=jnp.int32)[None, None, :]
    selector = jnp.sum(placing.astype(jnp.float32), axis=1).astype(jnp.bfloat16)
    filled = jnp.einsum("tr,td->rd", selector, tokens, preferred_element_type=jnp.float32)
    outgoing = filled.astype(jnp.bfloat16).reshape(experts, capacity, tokens.shape[1])
    full_rows = lax.all_gather(
        core_and_chips(outgoing, ("expert_0", "expert_1"), (1, 0), 0, 0),
        "tensor",
        axis=2,
        tiled=True,
    )
    width = full_rows.shape[2]
    flat = full_rows.reshape(-1, width)
    act = jnp.dot(flat, up_weight[0], preferred_element_type=jnp.float32)
    hidden = jax.nn.silu(act).astype(jnp.bfloat16)
    part = jnp.dot(hidden, down_weight[0], preferred_element_type=jnp.float32)
    partial_value = part.reshape(full_rows.shape[0], full_rows.shape[1], width)
    shares = summed_on_arrival(partial_value.astype(jnp.bfloat16), "tensor", 2).astype(jnp.bfloat16)
    returned = core_and_chips(shares, ("expert_0", "expert_1"), (1, 0), 0, 0)
    flat_rows = returned.reshape(experts * capacity, quarter_width)
    picked = jnp.take(flat_rows, position.reshape(-1), axis=0).reshape(
        tok_rows, top_count, quarter_width
    )
    gates = jax.nn.sigmoid(router_logits)
    weight = 2.5 * gates / jnp.sum(gates, axis=1, keepdims=True)
    mixed = jnp.sum(weight[:, :, None] * picked.astype(jnp.float32), axis=1)
    return mixed.astype(jnp.bfloat16)


def solution(mesh):
    split = Mesh(
        mesh.devices.reshape(mesh.shape["group"], 32, 2, mesh.shape["tensor"]),
        ("group", "expert_0", "expert_1", "tensor"),
    )
    return jax.shard_map(
        on_device,
        mesh=split,
        in_specs=(
            P(GROUP_EXPERT, "tensor"),
            P(GROUP_EXPERT, None),
            P(GROUP_EXPERT, None),
            P(EXPERT, None, "tensor"),
            P(EXPERT, "tensor", None),
        ),
        out_specs=P(GROUP_EXPERT, "tensor"),
        check_vma=False,
    )
```

profile of v0, /device:TPU:33, one launch (start us, length us, event | category | flops | bytes accessed | tf_op | source)
XLA Modules:
  0.0 381.4 jit_solution(5077829200390835637)
XLA Ops:
  6.6 0.9 copy.46
  7.5 0.1 convert_reduce_fusion.1
  7.6 0.7 select_reduce_fusion
  8.4 0.2 convert_reduce_fusion
  8.5 2.1 convolution_convert_fusion.1
  10.7 1.3 reshape_reshape_reshape.6
  12.0 0.4 copy.48
  12.4 45.4 %all_to_all.25 = bf16[32,2,1,6,1024]{4,0,3,2,1:T(8,128)(2,1)S(1)} all-to-all(bf16[32,2,1,6,1024]{4,0,3,2,1:T(8,128)(2,1)S(1)} %copy.48), channel_id=1, replica_groups=mesh['group'=2,'expert_0'=32,'expert_1'=2,'tensor'=4] {'expert_1'}, dimensions={1} | all-to-all | bytes 1572864 | tf_op jit(solution)/shard_map/all_to_all | solution.py:27
  57.9 0.8 copy.49
  58.7 91.0 %all_to_all.26 = bf16[32,2,1,6,1024]{4,1,3,2,0:T(2,128)(2,1)S(1)} all-to-all(bf16[32,2,1,6,1024]{4,1,3,2,0:T(2,128)(2,1)S(1)} %copy.49), channel_id=1, replica_groups=mesh['group'=2,'expert_0'=32,'expert_1'=2,'tensor'=4] {'expert_0'}, dimensions={0} | all-to-all | bytes 1572864 | tf_op jit(solution)/shard_map/all_to_all | solution.py:27
  149.7 0.5 copy.50
  150.3 1.2 reshape_reshape.6
  151.5 39.2 %all-gather.2.cloned.1.call-done = bf16[64,6,4096]{2,0,1:T(8,128)(2,1)} async-done(((bf16[64,6,1024]{2,0,1:T(8,128)(2,1)}), bf16[64,6,4096]{2,0,1:T(8,128)(2,1)}) %all-gather.2.cloned.1.call-update) | async-done | bytes 3145744 | tf_op jit(solution)/shard_map/all_gather | solution.py:60
  190.7 5.6 %copy.51 = bf16[64,6,4096]{2,1,0:T(8,128)(2,1)} copy(bf16[64,6,4096]{2,0,1:T(8,128)(2,1)} %all-gather.2.cloned.1.call-done) | data formatting | bytes 6291456 | tf_op jit(solution)/shard_map/all_gather | solution.py:60
  196.3 5.7 %reshape.64 = bf16[384,4096]{1,0:T(8,128)(2,1)} reshape(bf16[64,6,4096]{2,1,0:T(8,128)(2,1)} %copy.51) | data formatting | bytes 6291456 | tf_op jit(solution)/shard_map/reshape | solution.py:67
  202.0 3.5 multiply_convert_fusion
  205.7 1.0 convolution_convert_fusion
  206.7 0.4 copy.63
  207.1 40.0 %all_to_all.27 = bf16[4,64,6,1024]{3,1,2,0:T(8,128)(2,1)} all-to-all(bf16[4,64,6,1024]{3,1,2,0:T(8,128)(2,1)S(1)} %bitcast.30), channel_id=1, replica_groups=mesh['group'=2,'expert_0'=32,'expert_1'=2,'tensor'=4] {'tensor'}, dimensions={0} | all-to-all | bytes 6291456 | tf_op jit(solution)/shard_map/all_to_all | solution.py:39
  247.1 3.6 reduce_sum.61
  250.7 2.1 reshape_reshape.7
  252.9 0.2 copy.55
  253.1 6.0 %all_to_all.28 = bf16[32,2,1,6,1024]{4,0,3,2,1:T(8,128)(2,1)S(1)} all-to-all(bf16[32,2,1,6,1024]{4,0,3,2,1:T(8,128)(2,1)S(1)} %copy.55), channel_id=1, replica_groups=mesh['group'=2,'expert_0'=32,'expert_1'=2,'tensor'=4] {'expert_1'}, dimensions={1} | all-to-all | bytes 1572864 | tf_op jit(solution)/shard_map/all_to_all | solution.py:27
  259.1 1.7 copy.56
  260.7 23.2 %all-to-all-start.4 = ((bf16[32,2,1,6,1024]{4,1,3,2,0:T(2,128)(2,1)}), bf16[32,2,1,6,1024]{4,1,3,2,0:T(2,128)(2,1)S(1)}, u32[]{:S(2)}, u32[]{:S(2)}) async-start(bf16[32,2,1,6,1024]{4,1,3,2,0:T(2,128)(2,1)} %copy.56), calls=%async_computation.4 | async-start | bytes 1572864 | tf_op jit(solution)/shard_map/all_to_all | solution.py:27
  283.9 0.1 reshape.66
  284.1 0.1 copy.45
  284.2 85.5 %all-to-all-done.4 = bf16[32,2,1,6,1024]{4,1,3,2,0:T(2,128)(2,1)S(1)} async-done(((bf16[32,2,1,6,1024]{4,1,3,2,0:T(2,128)(2,1)}), bf16[32,2,1,6,1024]{4,1,3,2,0:T(2,128)(2,1)S(1)}, u32[]{:S(2)}, u32[]{:S(2)}) %all-to-all-start.4) | async-done | bytes 786464 | tf_op jit(solution)/shard_map/all_to_all | solution.py:27
  369.6 1.2 copy.57
  370.9 1.4 reshape_reshape_reshape.7
  372.3 1.2 gather_fusion
  373.5 1.1 multiply_reduce_fusion
  (14 shorter events, 0.3 us)
Async XLA Ops:
  6.5 199.1 %copy-start = (bf16[1,256,4096]{2,1,0:T(8,128)(2,1)S(1)}, bf16[1,256,4096]{2,1,0:T(8,128)(2,1)}, u32[]{:S(2)}) copy-start(bf16[1,256,4096]{2,1,0:T(8,128)(2,1)} %param.9) | copy-start | bytes 6291460
  6.6 184.2 %all-gather.2.cloned.1.call-start = ((), (), s32[]{:S(2)}) async-start(), calls=%async_computation.5 | async-start | bytes 3932160 | tf_op jit(solution)/shard_map/all_gather | solution.py:60
  252.8 31.2 %copy-start.1 = (f32[32,8]{0,1:T(8,128)S(1)}, f32[32,8]{0,1:T(8,128)}, u32[]{:S(2)}) copy-start(f32[32,8]{0,1:T(8,128)} %param.7) | copy-start | bytes 3076
  260.7 108.9 %all-to-all-start.4 = ((bf16[32,2,1,6,1024]{4,1,3,2,0:T(2,128)(2,1)}), bf16[32,2,1,6,1024]{4,1,3,2,0:T(2,128)(2,1)S(1)}, u32[]{:S(2)}, u32[]{:S(2)}) async-start(bf16[32,2,1,6,1024]{4,1,3,2,0:T(2,128)(2,1)} %copy.56), calls=%async_computation.4 | async-start | bytes 1572864 | tf_op jit(solution)/shard_map/all_to_all | solution.py:27
Sparse Core Ops, SparseCore 0:
  151.6 39.0 all-gather.1
where the time goes:
time: 382 us; the launch traced here: 381 us
  blocking collectives  182 us (48%)
  waiting for transfers between devices  125 us (33%)
  local copies, waits for them, and re-layouts  25 us (7%)
  starting transfers between devices  23.2 us (6%)
  between operations  13.6 us (4%)
  matrix products  6.63 us (2%)
  other arithmetic  5.84 us (2%)
    all_to_all x3, blocking collectives, exchange_in_order(): lax.all_to_all(pieces, axes[k], split_axis=k, concat_axis=k, tiled=True)  142 us
    all_to_all x1, waiting for transfers between devices, exchange_in_order(): lax.all_to_all(pieces, axes[k], split_axis=k, concat_axis=k, tiled=True)  85.5 us
    all_to_all x1, blocking collectives, summed_on_arrival(): lax.all_to_all(in_blocks(shard, dim, count), axis, 0, 0, tiled=True)  40 us
    all_gather x1, waiting for transfers between devices, on_device(): lax.all_gather(core_and_chips(outgoing, ('expert_0', 'expert_1'), (1, 0),...  39.2 us
    all_to_all x1, starting transfers between devices, exchange_in_order(): lax.all_to_all(pieces, axes[k], split_axis=k, concat_axis=k, tiled=True)  23.2 us
  transfers between devices with their start and end apart: 2, of which 2 were waited for; matrix products, arithmetic and copies ran while one was open for 0% of the time, Pallas kernels for 0%

commit v1 on v0

--- a/solution.py
+++ b/solution.py
@@ -57,12 +57,22 @@
     selector = jnp.sum(placing.astype(jnp.float32), axis=1).astype(jnp.bfloat16)
     filled = jnp.einsum("tr,td->rd", selector, tokens, preferred_element_type=jnp.float32)
     outgoing = filled.astype(jnp.bfloat16).reshape(experts, capacity, tokens.shape[1])
-    full_rows = lax.all_gather(
-        core_and_chips(outgoing, ("expert_0", "expert_1"), (1, 0), 0, 0),
-        "tensor",
-        axis=2,
-        tiled=True,
-    )
+    x = core_and_chips(outgoing, ("expert_0", "expert_1"), (1, 0), 0, 0)
+    ways, here, step = (lax.axis_size("tensor"), lax.axis_index("tensor"), x.shape[2])
+    shape_2 = [n * ways if d == 2 else n for d, n in enumerate(x.shape)]
+    full = lax.dynamic_update_slice_in_dim(jnp.zeros(shape_2, x.dtype), x, here * step, axis=2)
+    going_up = going_down = x
+    for far in range(1, ways // 2 + 1):
+        going_up = lax.ppermute(going_up, "tensor", [(d, (d + 1) % ways) for d in range(ways)])
+        full = lax.dynamic_update_slice_in_dim(full, going_up, (here - far) % ways * step, axis=2)
+        if 2 * far < ways:
+            going_down = lax.ppermute(
+                going_down, "tensor", [(d, (d - 1) % ways) for d in range(ways)]
+            )
+            full = lax.dynamic_update_slice_in_dim(
+                full, going_down, (here + far) % ways * step, axis=2
+            )
+    full_rows = full
     width = full_rows.shape[2]
     flat = full_rows.reshape(-1, width)
     act = jnp.dot(flat, up_weight[0], preferred_element_type=jnp.float32)

time: 382 us -> 352 us (0.921)
  waiting for transfers between devices: 125 us -> 109 us
  between operations: 13.6 us -> 0.24 us
  starting transfers between devices: 23.2 us -> 15.4 us
  local copies, waits for them, and re-layouts: 25 us -> 32 us
    all_gather x1 -> x0, waiting for transfers between devices: 39.2 us -> none  [on_device(): lax.all_gather(core_and_chips(outgoing, ('expert_0', 'expert_1'), (1, 0),...]
    ppermute x0 -> x3, waiting for transfers between devices: none -> 23.4 us  [the longest x2 23.4 us: on_device(): lax.ppermute(going_up, 'tensor', [(d, (d + 1) % ways) for d in range(ways)])]
    all_to_all x1, starting transfers between devices: 23.2 us -> 6.66 us  [exchange_in_order(): lax.all_to_all(pieces, axes[k], split_axis=k, concat_axis=k, tiled=True)]
    ppermute x0 -> x3, starting transfers between devices: none -> 8.71 us  [the longest x2 5.22 us: on_device(): lax.ppermute(going_up, 'tensor', [(d, (d + 1) % ways) for d in range(ways)])]
    dynamic_update_slice x0 -> x4, local copies, waits for them, and re-layouts: none -> 8.19 us  [the longest x2 4.04 us: on_device(): lax.dynamic_update_slice_in_dim(full, going_up, (here - far) % ways * ste...]
    all_gather x1 -> x0, local copies, waits for them, and re-layouts: 5.57 us -> none  [on_device(): lax.all_gather(core_and_chips(outgoing, ('expert_0', 'expert_1'), (1, 0),...]
  transfers between devices with their start and end apart: 2 -> 4, of which waited for: 2 -> 3; matrix products, arithmetic and copies ran while one was open for 0% -> 3% of each run, Pallas kernels for 0% -> 0%
where the time goes in v1:
time: 352 us; the launch traced here: 351 us
  blocking collectives  182 us (52%)
  waiting for transfers between devices  109 us (31%)
  local copies, waits for them, and re-layouts  32 us (9%)
  starting transfers between devices  15.4 us (4%)
  matrix products  6.63 us (2%)
  other arithmetic  5.84 us (2%)
    all_to_all x3, blocking collectives, exchange_in_order(): lax.all_to_all(pieces, axes[k], split_axis=k, concat_axis=k, tiled=True)  144 us
    all_to_all x1, waiting for transfers between devices, exchange_in_order(): lax.all_to_all(pieces, axes[k], split_axis=k, concat_axis=k, tiled=True)  85.5 us
    all_to_all x1, blocking collectives, summed_on_arrival(): lax.all_to_all(in_blocks(shard, dim, count), axis, 0, 0, tiled=True)  37.9 us
    ppermute x2, waiting for transfers between devices, on_device(): lax.ppermute(going_up, 'tensor', [(d, (d + 1) % ways) for d in range(ways)])  23.4 us
  transfers between devices with their start and end apart: 4, of which 3 were waited for; matrix products, arithmetic and copies ran while one was open for 3% of the time, Pallas kernels for 0%

profile of v1, /device:TPU:33, one launch (start us, length us, event | category | flops | bytes accessed | tf_op | source)
XLA Modules:
  0.0 351.4 jit_solution(12217453222511121391)
XLA Ops:
  0.0 0.9 copy.53
  2.0 2.1 convolution_convert_fusion.1
  4.1 1.3 reshape_reshape_reshape.6
  5.9 45.4 %all_to_all.25 = bf16[32,2,1,6,1024]{4,0,3,2,1:T(8,128)(2,1)S(1)} all-to-all(bf16[32,2,1,6,1024]{4,0,3,2,1:T(8,128)(2,1)S(1)} %copy.55), channel_id=1, replica_groups=mesh['group'=2,'expert_0'=32,'expert_1'=2,'tensor'=4] {'expert_1'}, dimensions={1} | all-to-all | bytes 1572864 | tf_op jit(solution)/shard_map/all_to_all | solution.py:27
  51.3 0.8 copy.56
  52.1 91.0 %all_to_all.26 = bf16[32,2,1,6,1024]{4,1,3,2,0:T(2,128)(2,1)S(1)} all-to-all(bf16[32,2,1,6,1024]{4,1,3,2,0:T(2,128)(2,1)S(1)} %copy.56), channel_id=1, replica_groups=mesh['group'=2,'expert_0'=32,'expert_1'=2,'tensor'=4] {'expert_0'}, dimensions={0} | all-to-all | bytes 1572864 | tf_op jit(solution)/shard_map/all_to_all | solution.py:27
  143.2 1.4 copy.57
  144.6 2.3 reshape_reshape.6
  146.9 3.3 collective-permute-start
  150.1 3.5 collective-permute-start.1
  153.7 14.3 %collective-permute-done = bf16[64,6,1024]{2,0,1:T(8,128)(2,1)} collective-permute-done((bf16[64,6,1024]{2,0,1:T(8,128)(2,1)S(1)}, bf16[64,6,1024]{2,0,1:T(8,128)(2,1)}, u32[]{:S(2)}, u32[]{:S(2)}) %collective-permute-start) | collective-permute-done | bytes 786464 | tf_op jit(solution)/shard_map/ppermute | solution.py:66
  168.0 1.9 collective-permute-start.2
  170.0 2.4 broadcast_in_dim.13
  172.4 1.5 copy_dynamic-update-slice_fusion.3
  173.9 2.6 copy_dynamic-update-slice_fusion.2
  176.5 2.7 copy_dynamic-update-slice_fusion.1
  179.1 9.1 %collective-permute-done.2 = bf16[64,6,1024]{2,0,1:T(8,128)(2,1)S(1)} collective-permute-done((bf16[64,6,1024]{2,0,1:T(8,128)(2,1)}, bf16[64,6,1024]{2,0,1:T(8,128)(2,1)S(1)}, u32[]{:S(2)}, u32[]{:S(2)}) %collective-permute-start.2) | collective-permute-done | bytes 786464 | tf_op jit(solution)/shard_map/ppermute | solution.py:66
  188.2 1.5 copy_dynamic-update-slice_fusion
  189.7 5.7 %reshape.64 = bf16[384,4096]{1,0:T(8,128)(2,1)} reshape(bf16[64,6,4096]{2,1,0:T(8,128)(2,1)} %copy_dynamic-update-slice_fusion) | data formatting | bytes 6291456 | tf_op jit(solution)/shard_map/reshape | solution.py:77
  195.4 3.5 %multiply_convert_fusion = bf16[384,256]{1,0:T(8,128)(2,1)S(1)} fusion(bf16[384,4096]{1,0:T(8,128)(2,1)} %reshape.64, bf16[1,4096,256]{2,1,0:T(8,128)(2,1)} %param.8), kind=kOutput, calls=%fused_computation.13 | convolution fusion | flops 805797888 | bytes 5439488 | tf_op jit(solution)/shard_map/dot_general | solution.py:78
  199.0 1.0 convolution_convert_fusion
  200.5 37.9 %all_to_all.27 = bf16[4,64,6,1024]{3,1,2,0:T(8,128)(2,1)} all-to-all(bf16[4,64,6,1024]{3,1,2,0:T(8,128)(2,1)S(1)} %bitcast.30), channel_id=1, replica_groups=mesh['group'=2,'expert_0'=32,'expert_1'=2,'tensor'=4] {'tensor'}, dimensions={0} | all-to-all | bytes 6291456 | tf_op jit(solution)/shard_map/all_to_all | solution.py:39
  238.4 3.6 %reduce_sum.61 = bf16[64,6,1024]{2,0,1:T(8,128)(2,1)} reduce(bf16[4,64,6,1024]{3,1,2,0:T(8,128)(2,1)} %all_to_all.27, bf16[]{:T(256)} %constant.59.clone.1), dimensions={0}, to_apply=%region_5.6 | reduce | flops 1179648 | bytes 3932162 | tf_op jit(solution)/shard_map/reduce_sum | solution.py:40
  242.0 2.1 reshape_reshape.7
  244.4 8.0 %all_to_all.28 = bf16[32,2,1,6,1024]{4,0,3,2,1:T(8,128)(2,1)S(1)} all-to-all(bf16[32,2,1,6,1024]{4,0,3,2,1:T(8,128)(2,1)S(1)} %copy.65), channel_id=1, replica_groups=mesh['group'=2,'expert_0'=32,'expert_1'=2,'tensor'=4] {'expert_1'}, dimensions={1} | all-to-all | bytes 1572864 | tf_op jit(solution)/shard_map/all_to_all | solution.py:27
  252.4 1.7 copy.66
  254.1 6.7 %all-to-all-start.4 = ((bf16[32,2,1,6,1024]{4,1,3,2,0:T(2,128)(2,1)}), bf16[32,2,1,6,1024]{4,1,3,2,0:T(2,128)(2,1)S(1)}, u32[]{:S(2)}, u32[]{:S(2)}) async-start(bf16[32,2,1,6,1024]{4,1,3,2,0:T(2,128)(2,1)} %copy.66), calls=%async_computation.4 | async-start | bytes 1572864 | tf_op jit(solution)/shard_map/all_to_all | solution.py:27
  261.0 85.5 %all-to-all-done.4 = bf16[32,2,1,6,1024]{4,1,3,2,0:T(2,128)(2,1)S(1)} async-done(((bf16[32,2,1,6,1024]{4,1,3,2,0:T(2,128)(2,1)}), bf16[32,2,1,6,1024]{4,1,3,2,0:T(2,128)(2,1)S(1)}, u32[]{:S(2)}, u32[]{:S(2)}) %all-to-all-start.4) | async-done | bytes 786464 | tf_op jit(solution)/shard_map/all_to_all | solution.py:27
  346.5 1.2 copy.67
  347.7 1.4 reshape_reshape_reshape.7
  349.1 1.2 gather_fusion
  350.3 1.1 multiply_reduce_fusion
  (21 shorter events, 2.4 us)
Async XLA Ops:
  0.0 199.0 %copy-start = (bf16[1,256,4096]{2,1,0:T(8,128)(2,1)S(1)}, bf16[1,256,4096]{2,1,0:T(8,128)(2,1)}, u32[]{:S(2)}) copy-start(bf16[1,256,4096]{2,1,0:T(8,128)(2,1)} %param.9) | copy-start | bytes 6291460
  146.9 21.2 %collective-permute-start = (bf16[64,6,1024]{2,0,1:T(8,128)(2,1)S(1)}, bf16[64,6,1024]{2,0,1:T(8,128)(2,1)}, u32[]{:S(2)}, u32[]{:S(2)}) collective-permute-start(bf16[64,6,1024]{2,0,1:T(8,128)(2,1)S(1)} %reshape_reshape.6), channel_id=1, source_target_pairs={{0,1},{1,2},{2,3},{3,0},{4,5},{5,6},{6,7},{7,4},{8,9},{9,10},{10,1... | collective-permute-start | bytes 2359304 | tf_op jit(solution)/shard_map/ppermute | solution.py:66
  150.1 26.3 %collective-permute-start.1 = (bf16[64,6,1024]{2,0,1:T(8,128)(2,1)S(1)}, bf16[64,6,1024]{2,0,1:T(8,128)(2,1)}, u32[]{:S(2)}, u32[]{:S(2)}) collective-permute-start(bf16[64,6,1024]{2,0,1:T(8,128)(2,1)S(1)} %reshape_reshape.6), channel_id=1, source_target_pairs={{0,3},{1,0},{2,1},{3,2},{4,7},{5,4},{6,5},{7,6},{8,11},{9,8},{10,9... | collective-permute-start | bytes 2359304 | tf_op jit(solution)/shard_map/ppermute | solution.py:69
  168.0 20.2 %collective-permute-start.2 = (bf16[64,6,1024]{2,0,1:T(8,128)(2,1)}, bf16[64,6,1024]{2,0,1:T(8,128)(2,1)S(1)}, u32[]{:S(2)}, u32[]{:S(2)}) collective-permute-start(bf16[64,6,1024]{2,0,1:T(8,128)(2,1)} %collective-permute-done), channel_id=1, source_target_pairs={{0,1},{1,2},{2,3},{3,0},{4,5},{5,6},{6,7},{7,4},{8,9},{9,10},{10,1... | collective-permute-start | bytes 2359304 | tf_op jit(solution)/shard_map/ppermute | solution.py:66
  244.2 16.6 %copy-start.1 = (f32[32,8]{0,1:T(8,128)S(1)}, f32[32,8]{0,1:T(8,128)}, u32[]{:S(2)}) copy-start(f32[32,8]{0,1:T(8,128)} %param.7) | copy-start | bytes 3076
  254.1 92.4 %all-to-all-start.4 = ((bf16[32,2,1,6,1024]{4,1,3,2,0:T(2,128)(2,1)}), bf16[32,2,1,6,1024]{4,1,3,2,0:T(2,128)(2,1)S(1)}, u32[]{:S(2)}, u32[]{:S(2)}) async-start(bf16[32,2,1,6,1024]{4,1,3,2,0:T(2,128)(2,1)} %copy.66), calls=%async_computation.4 | async-start | bytes 1572864 | tf_op jit(solution)/shard_map/all_to_all | solution.py:27
